TPU v7x, 32 devices: a whole 2x2x4 slice. The times are simulated.
32 devices in a mesh: dp: 4 (over x, core), tensor: 8 (over z, y).
Axes of the slice: x: 2, y: 2, z: 4, core: 2. Of those that a mesh axis runs over, the one named last changes fastest.
Arguments:
- attn_ctx: bfloat16 [2048, 8192], P('dp', 'tensor'), may hold values from -6 to 6
- w_out: bfloat16 [8192, 8192], P('tensor'), may hold values from -0.09375 to 0.09375
- resid: bfloat16 [2048, 8192], P(('dp', 'tensor')), may hold values from -6 to 6
- teacher_gain: bfloat16 [8192], replicated, may hold values from 0.25 to 1.75
- dest_row: int32 [2048], replicated, may hold values from 0 to 2047, as said below
- student_in: bfloat16 [2048, 4096], P('dp', 'tensor'), may hold values from -6 to 6
- student_gain: bfloat16 [4096], replicated, may hold values from 0.25 to 1.75
- w_gate: bfloat16 [4096, 14336], P('dp', 'tensor'), may hold values from -0.09375 to 0.09375
- w_up: bfloat16 [4096, 14336], P('dp', 'tensor'), may hold values from -0.09375 to 0.09375
- w_down: bfloat16 [14336, 4096], P('tensor', 'dp'), may hold values from -0.0625 to 0.0625
- proj: bfloat16 [4096, 8192], P('dp', 'tensor'), may hold values from -0.09375 to 0.09375
Outputs:
- student_out: bfloat16 [2048, 4096], P('dp', 'tensor')
- row_loss: float32 [2048], P('dp')
- residue: float32 [2048, 8192], P('dp', 'tensor')
Inputs may be any that keep to these rules, and one draw needn't show every extreme that they name: A permutation of the rows; of the 64 rows i in one aligned block of teacher rows, at most 32 have dest_row[i] in any one tile of 512 student rows, and some tile receives exactly 32 of them.
All inputs are finite; a program needn't handle non-finite values.
Results may differ from a plain program's by a relative error of at most 0.012.
Values may be sent and summed in bfloat16 or wider, within the bound.
A program may use at most 192 MiB of HBM per device.

v0:
```python
import jax
import jax.numpy as jnp
from jax import lax
from jax.sharding import PartitionSpec as P

HT = 8192


def local(
    attn_ctx,
    w_out,
    resid,
    teacher_gain,
    dest_row,
    student_in,
    student_gain,
    w_gate,
    w_up,
    w_down,
    proj,
):
    tensor_count = lax.axis_size("tensor")
    group_count = lax.axis_size("dp")
    tile_rows = attn_ctx.shape[0]
    own_rows = resid.shape[0]
    portion = attn_ctx
    summed = lax.psum_scatter(
        jnp.dot(portion, w_out, preferred_element_type=jnp.float32).astype(jnp.bfloat16),
        "tensor",
        scatter_dimension=0,
        tiled=True,
    ).astype(jnp.float32)
    teacher_hidden = resid.astype(jnp.float32) + summed
    square_mean = jnp.mean(teacher_hidden * teacher_hidden, axis=1, keepdims=True)
    teacher_final = (
        teacher_hidden * lax.rsqrt(square_mean + 1e-06) * teacher_gain.astype(jnp.float32)
    ).astype(jnp.bfloat16)
    capacity = 2 * own_rows // group_count
    source_count = group_count * tensor_count
    group_ids = (dest_row // tile_rows).reshape(source_count, own_rows)
    onehot = (group_ids[:, :, None] == jnp.arange(group_count)[None, None, :]).astype(jnp.int32)
    slot_index = jnp.sum((jnp.cumsum(onehot, 1) - onehot) * onehot, 2)
    my_source = lax.axis_index("dp") * tensor_count + lax.axis_index("tensor")
    own_groups = lax.dynamic_index_in_dim(group_ids, my_source, 0, keepdims=False)
    own_slots = lax.dynamic_index_in_dim(slot_index, my_source, 0, keepdims=False)
    target_slot = own_groups * capacity + own_slots
    selector = (target_slot[None, :] == jnp.arange(group_count * capacity)[:, None]).astype(
        jnp.bfloat16
    )
    packed = jnp.dot(selector, teacher_final, preferred_element_type=jnp.float32).astype(
        jnp.bfloat16
    )
    col_width = teacher_final.shape[1] // tensor_count
    send_blocks = packed.reshape(group_count, capacity, tensor_count, col_width).transpose(
        0, 2, 1, 3
    )
    arrived = lax.all_to_all(
        lax.all_to_all(send_blocks, "dp", split_axis=0, concat_axis=0, tiled=True),
        "tensor",
        split_axis=1,
        concat_axis=1,
        tiled=True,
    )
    flattened = arrived.reshape(source_count * capacity, col_width)
    arrival_index = (jnp.arange(source_count)[:, None] * capacity + slot_index).reshape(-1)
    inverse = jnp.zeros(dest_row.shape, jnp.int32).at[dest_row].set(arrival_index)
    own_arrivals = lax.dynamic_slice_in_dim(inverse, lax.axis_index("dp") * tile_rows, tile_rows, 0)
    target = jnp.take(flattened, own_arrivals, axis=0)
    gathered = lax.all_gather(student_in, "tensor", axis=1, tiled=True)
    x_full = gathered.astype(jnp.float32)
    student_mean = jnp.mean(x_full * x_full, axis=1, keepdims=True)
    normed = (x_full * lax.rsqrt(student_mean + 1e-05) * student_gain.astype(jnp.float32)).astype(
        jnp.bfloat16
    )

    def add_rows(portion):
        return jnp.dot(normed, portion, preferred_element_type=jnp.float32)

    gate_acts = add_rows(lax.all_gather(w_gate, "dp", axis=0, tiled=True))
    up_acts = add_rows(lax.all_gather(w_up, "dp", axis=0, tiled=True))
    hidden = (jax.nn.silu(gate_acts) * up_acts).astype(jnp.bfloat16)
    partial_sum = jnp.dot(
        hidden, lax.all_gather(w_down, "dp", axis=1, tiled=True), preferred_element_type=jnp.float32
    )
    local_cols = student_in.shape[1]
    mlp_sum = lax.psum(partial_sum.astype(jnp.bfloat16), "tensor").astype(jnp.float32)
    out_full = (x_full + mlp_sum).astype(jnp.bfloat16)
    out_local = lax.dynamic_slice_in_dim(
        out_full, lax.axis_index("tensor") * local_cols, local_cols, 1
    )
    pred = jnp.dot(
        out_full, lax.all_gather(proj, "dp", axis=0, tiled=True), preferred_element_type=jnp.float32
    )
    residue = pred - target.astype(jnp.float32)
    row_error = jnp.sum(residue * residue, axis=1)
    row_loss = lax.psum(row_error, "tensor") / HT
    return (out_local, row_loss, residue)


def solution(mesh):
    placed = (
        P("dp", "tensor"),
        P("tensor", None),
        P(("dp", "tensor"), None),
        P(),
        P(),
        P("dp", "tensor"),
        P(),
        P("dp", "tensor"),
        P("dp", "tensor"),
        P("tensor", "dp"),
        P("dp", "tensor"),
    )
    return jax.shard_map(
        local,
        mesh=mesh,
        in_specs=placed,
        out_specs=(P("dp", "tensor"), P("dp"), P("dp", "tensor")),
        check_vma=False,
    )
```

profile of v0, /device:TPU:0, one launch (start us, length us, event | category | flops | bytes accessed | tf_op | source)
XLA Modules:
  0.0 813.1 jit_solution(8429802727703756237)
XLA Ops:
  10.0 16.8 %convolution_convert_fusion = bf16[512,8192]{1,0:T(8,128)(2,1)} fusion(bf16[512,1024]{1,0:T(8,128)(2,1)S(1)} %copy-done, bf16[1024,8192]{1,0:T(8,128)(2,1)} %param.12), kind=kOutput, calls=%fused_computation.5 | convolution fusion | flops 8594128896 | bytes 26214400 | tf_op jit(solution)/shard_map/dot_general | solution.py:28
  27.5 59.9 %all-gather.6.cloned.1.call-done = bf16[512,4096]{1,0:T(8,128)(2,1)} async-done(((bf16[512,512]{1,0:T(8,128)(2,1)}), bf16[512,4096]{1,0:T(8,128)(2,1)}) %all-gather.6.cloned.1.call-update) | async-done | bytes 4194320 | tf_op jit(solution)/shard_map/all_gather | solution.py:69
  87.4 3.1 fusion
  90.5 90.7 %all-gather.8.cloned.1.call-done = bf16[4096,1792]{1,0:T(8,128)(2,1)} async-done(((bf16[1024,1792]{1,0:T(8,128)(2,1)}), bf16[4096,1792]{1,0:T(8,128)(2,1)}) %all-gather.8.cloned.1.call-update) | async-done | bytes 14680080 | tf_op jit(solution)/shard_map/all_gather | solution.py:79
  181.2 14.7 %fusion.11 = f32[512,1792]{1,0:T(8,128)} fusion(bf16[4096,1792]{1,0:T(8,128)(2,1)} %all-gather.8.cloned.1.call-done, bf16[512,4096]{1,0:T(8,128)(2,1)} %all-gather.6.cloned.1.call-done, f32[4096]{0:T(1024)S(1)} %convert_element_type.47, f32[512]{0:T(512)S(1)} %add_rsqrt_fusion), kind=kOutput, calls=%fused_computation.23 | convolution fusion | flops 7524581376 | bytes 22562816 | tf_op jit(solution)/shard_map/dot_general | solution.py:77
  195.8 80.9 %all-gather.12.cloned.1.call-done = bf16[1792,4096]{1,0:T(8,128)(2,1)} async-done(((bf16[1792,1024]{1,0:T(8,128)(2,1)}), bf16[1792,4096]{1,0:T(8,128)(2,1)}) %all-gather.12.cloned.1.call-update) | async-done | bytes 14680080 | tf_op jit(solution)/shard_map/all_gather | solution.py:83
  276.8 95.4 %all-gather.10.cloned.1.call-done = bf16[4096,1792]{1,0:T(8,128)(2,1)} async-done(((bf16[1024,1792]{1,0:T(8,128)(2,1)}), bf16[4096,1792]{1,0:T(8,128)(2,1)}) %all-gather.10.cloned.1.call-update) | async-done | bytes 14680080 | tf_op jit(solution)/shard_map/all_gather | solution.py:80
  372.2 28.8 %convolution_convert_fusion.2 = bf16[512,4096]{1,0:T(8,128)(2,1)} fusion(bf16[1792,4096]{1,0:T(8,128)(2,1)} %all-gather.12.cloned.1.call-done, f32[512,1792]{1,0:T(8,128)} %fusion.11, bf16[4096,1792]{1,0:T(8,128)(2,1)} %all-gather.10.cloned.1.call-done, bf16[512,4096]{1,0:T(8,128)(2,1)} %all-gather.6.cloned.1.call-done, f32[4096]{0:T(1024)S(1)} %convert_element_type.47, ...), kind=kOutput, calls=%fused_computation.11 | convolution fusion | flops 15048376320 | bytes 41437184 | tf_op jit(solution)/shard_map/dot_general | solution.py:82
  402.0 1.7 select_reduce_fusion
  403.9 119.3 %reduce-scatter.2.cloned.1.call-done = bf16[64,8192]{1,0:T(8,128)(2,1)} async-done(((bf16[512,8192]{1,0:T(8,128)(2,1)}), bf16[64,8192]{1,0:T(8,128)(2,1)}) %reduce-scatter.2.cloned.1.call-update) | async-done | bytes 1048592 | tf_op jit(solution)/shard_map/reduce_scatter | solution.py:27
  523.2 1.7 multiply_reduce_fusion.1
  524.9 2.0 convolution_convert_fusion.1
  529.5 28.2 %all_to_all.10 = bf16[4,8,32,1024]{3,2,1,0:T(8,128)(2,1)S(1)} all-to-all(bf16[4,8,32,1024]{3,2,1,0:T(8,128)(2,1)S(1)} %bitcast.17), channel_id=1, replica_groups=mesh['dp'=4,'tensor'=8] {'dp'}, dimensions={0} | all-to-all | bytes 4194304 | tf_op jit(solution)/shard_map/all_to_all | solution.py:58
  559.1 4.3 all-to-all-start.1
  563.7 8.3 %scatter_custom_fusion = s32[2048]{0:T(1024)S(1)} fusion(s32[2048]{0:T(1024)S(1)} %get-tuple-element.5, s32[2048]{0:T(1024)S(1)} %reshape.60, s32[]{:T(128)} %constant.62.clone.1), kind=kCustom, calls=%fused_computation.43 | custom fusion | bytes 8196 | tf_op jit(solution)/shard_map/scatter | solution.py:66
  572.1 64.3 %all-to-all-done.1 = bf16[4,8,32,1024]{3,2,0,1:T(8,128)(2,1)} async-done(((bf16[4,8,32,1024]{3,2,0,1:T(8,128)(2,1)}), bf16[4,8,32,1024]{3,2,0,1:T(8,128)(2,1)}, u32[]{:S(2)}, u32[]{:S(2)}) %all-to-all-start.1) | async-done | bytes 2097184 | tf_op jit(solution)/shard_map/all_to_all | solution.py:57
  636.5 1.8 copy.34
  638.3 2.8 gather_fusion
  641.1 73.8 %all-reduce.2.cloned.1.call-done = bf16[512,4096]{1,0:T(8,128)(2,1)} async-done(((bf16[512,4096]{1,0:T(8,128)(2,1)}), bf16[512,4096]{1,0:T(8,128)(2,1)}) %all-reduce.2.cloned.1.call-update) | async-done | bytes 4194320 | tf_op jit(solution)/shard_map/psum | solution.py:86
  714.9 5.0 fusion.3
  719.9 1.9 copy-done.2
  722.7 51.0 %all-gather.14.cloned.1.call-done = bf16[4096,1024]{1,0:T(8,128)(2,1)} async-done(((bf16[1024,1024]{1,0:T(8,128)(2,1)}), bf16[4096,1024]{1,0:T(8,128)(2,1)}) %all-gather.14.cloned.1.call-update) | async-done | bytes 8388624 | tf_op jit(solution)/shard_map/all_gather | solution.py:92
  773.7 10.6 %multiply_reduce_fusion = (f32[512]{0:T(512)S(1)}, f32[512,1024]{1,0:T(8,128)}) fusion(bf16[512,1024]{1,0:T(8,128)(2,1)S(1)} %copy-done.4, pred[512]{0:T(512)(128)(4,1)S(1)} %get-tuple-element.3, bf16[512,4096]{1,0:T(8,128)(2,1)} %copy-done.2, bf16[4096,1024]{1,0:T(8,128)(2,1)} %all-gather.14.cloned.1.call-done), kind=kOutput, calls=%fused_computation.14 | convolution fusion | flops 4297588224 | bytes 15731200 | tf_op jit(solution)/shard_map/dot_general | solution.py:91
  784.3 21.3 %psum.15 = f32[512]{0:T(512)S(1)} all-reduce(f32[512]{0:T(512)S(1)} %get-tuple-element.7), channel_id=1, replica_groups=mesh['dp'=4,'tensor'=8] {'tensor'}, use_global_device_ids=true, to_apply=%region_8.9 | all-reduce | flops 512 | bytes 4096 | tf_op jit(solution)/shard_map/psum | solution.py:96
  (48 shorter events, 10.4 us)
Async XLA Ops:
  7.2 2.9 copy-start
  7.2 80.2 %all-gather.6.cloned.1.call-start = ((), (), s32[]{:S(2)}) async-start(), calls=%async_computation.3 | async-start | bytes 4718592 | tf_op jit(solution)/shard_map/all_gather | solution.py:69
  7.9 173.3 %all-gather.8.cloned.1.call-start = ((), (), s32[]{:S(2)}) async-start(), calls=%async_computation.4 | async-start | bytes 18350080 | tf_op jit(solution)/shard_map/all_gather | solution.py:79
  8.7 268.1 %all-gather.12.cloned.1.call-start = ((), (), s32[]{:S(2)}) async-start(), calls=%async_computation.6 | async-start | bytes 18350080 | tf_op jit(solution)/shard_map/all_gather | solution.py:83
  9.4 362.8 %all-gather.10.cloned.1.call-start = ((), (), s32[]{:S(2)}) async-start(), calls=%async_computation.5 | async-start | bytes 18350080 | tf_op jit(solution)/shard_map/all_gather | solution.py:80
  10.0 513.2 %reduce-scatter.2.cloned.1.call-start = ((), (), s32[]{:S(2)}) async-start(), calls=%async_computation.9 | async-start | bytes 9437184 | tf_op jit(solution)/shard_map/reduce_scatter | solution.py:27
  26.8 0.7 copy-start.6
  26.8 688.0 %all-reduce.2.cloned.1.call-start = ((), (), s32[]{:S(2)}) async-start(), calls=%async_computation.7 | async-start | bytes 8388608 | tf_op jit(solution)/shard_map/psum | solution.py:86
  401.0 0.8 copy-start.5
  401.0 0.8 copy-start.7
  401.0 122.2 %copy-start.3 = (bf16[64,8192]{1,0:T(8,128)(2,1)S(1)}, bf16[64,8192]{1,0:T(8,128)(2,1)}, u32[]{:S(2)}) copy-start(bf16[64,8192]{1,0:T(8,128)(2,1)} %param.13) | copy-start | bytes 3145732
  401.0 372.7 %all-gather.14.cloned.1.call-start = ((), (), s32[]{:S(2)}) async-start(), calls=%async_computation.8 | async-start | bytes 10485760 | tf_op jit(solution)/shard_map/all_gather | solution.py:92
  559.1 77.3 %all-to-all-start.1 = ((bf16[4,8,32,1024]{3,2,0,1:T(8,128)(2,1)}), bf16[4,8,32,1024]{3,2,0,1:T(8,128)(2,1)}, u32[]{:S(2)}, u32[]{:S(2)}) async-start(bf16[4,8,32,1024]{3,2,0,1:T(8,128)(2,1)} %copy.33), calls=%async_computation.2 | async-start | bytes 4194304 | tf_op jit(solution)/shard_map/all_to_all | solution.py:57
  641.1 132.7 %copy-start.4 = (bf16[512,1024]{1,0:T(8,128)(2,1)S(1)}, bf16[512,1024]{1,0:T(8,128)(2,1)}, u32[]{:S(2)}) copy-start(bf16[512,1024]{1,0:T(8,128)(2,1)} %gather_fusion) | copy-start | bytes 3145732
  719.9 2.0 copy-start.2
  773.7 32.5 %copy-start.1 = (bf16[512,1024]{1,0:T(8,128)(2,1)S(1)}, bf16[512,1024]{1,0:T(8,128)(2,1)}, u32[]{:S(2)}) copy-start(bf16[512,1024]{1,0:T(8,128)(2,1)} %param.11) | copy-start | bytes 3145732
Sparse Core Ops, SparseCore 0:
  10.0 77.3 all-gather.5
  89.0 92.1 all-gather.7
  182.8 93.9 all-gather.11
  278.2 93.9 all-gather.9
  375.7 147.4 reduce-scatter.1
  526.7 188.0 all-reduce.1
  716.4 57.2 all-gather.13
where the time goes:
time: 814 us; the launch traced here: 813 us
  waiting for transfers between devices  639 us (79%)
  matrix products  72.8 us (9%)
  blocking collectives  49.5 us (6%)
  local copies, waits for them, and re-layouts  20.5 us (3%)
  between operations  14.3 us (2%)
  other arithmetic  12.4 us (2%)
    reduce_scatter x1, waiting for transfers between devices, local(): lax.psum_scatter(jnp.dot(portion, w_out, preferred_element_type=jnp.float...  119 us
    all_gather x1, waiting for transfers between devices, local(): up_acts = add_rows(lax.all_gather(w_up, 'dp', axis=0, tiled=True))  95.4 us
    all_gather x1, waiting for transfers between devices, local(): gate_acts = add_rows(lax.all_gather(w_gate, 'dp', axis=0, tiled=True))  90.7 us
    all_gather x1, waiting for transfers between devices, local(): lax.all_gather(w_down, 'dp', axis=1, tiled=True)  80.9 us
    psum x1, waiting for transfers between devices, local(): lax.psum(partial_sum.astype(jnp.bfloat16), 'tensor').astype(jnp.float32)  73.8 us
    all_to_all x1, waiting for transfers between devices, local(): lax.all_to_all(lax.all_to_all(send_blocks, 'dp', split_axis=0, concat_axi...  64.3 us
    all_gather x1, waiting for transfers between devices, local(): gathered = lax.all_gather(student_in, 'tensor', axis=1, tiled=True)  59.9 us
    all_gather x1, waiting for transfers between devices, local(): lax.all_gather(proj, 'dp', axis=0, tiled=True)  51 us
  transfers between devices with their start and end apart: 8, of which 8 were waited for; matrix products, arithmetic and copies ran while one was open for 11% of the time, Pallas kernels for 0%

commit v1 on v0

--- a/solution.py
+++ b/solution.py
@@ -2,8 +2,13 @@
 import jax.numpy as jnp
 from jax import lax
 from jax.sharding import PartitionSpec as P
+from jax.lax import all_gather
 
 HT = 8192
+
+
+def plan_field(sample):
+    return jnp.sum(all_gather(sample, axis_name="tensor"), 0)
 
 
 def local(
@@ -83,7 +88,7 @@
         hidden, lax.all_gather(w_down, "dp", axis=1, tiled=True), preferred_element_type=jnp.float32
     )
     local_cols = student_in.shape[1]
-    mlp_sum = lax.psum(partial_sum.astype(jnp.bfloat16), "tensor").astype(jnp.float32)
+    mlp_sum = plan_field(partial_sum.astype(jnp.bfloat16)).astype(jnp.float32)
     out_full = (x_full + mlp_sum).astype(jnp.bfloat16)
     out_local = lax.dynamic_slice_in_dim(
         out_full, lax.axis_index("tensor") * local_cols, local_cols, 1

time: 814 us -> 1280 us (1.57)
  waiting for transfers between devices: 639 us -> 1090 us
  other arithmetic: 12.4 us -> 28.3 us
    all_gather x0 -> x1, waiting for transfers between devices: none -> 546 us  [plan_field(): return jnp.sum(all_gather(sample, axis_name='tensor'), 0)]
    psum x1 -> x0, waiting for transfers between devices: 73.8 us -> none  [local(): lax.psum(partial_sum.astype(jnp.bfloat16), 'tensor').astype(jnp.float32)]
    reduce_sum x0 -> x1, other arithmetic: none -> 15.8 us  [plan_field(): return jnp.sum(all_gather(sample, axis_name='tensor'), 0)]
    all_gather x1, waiting for transfers between devices: 51 us -> 36.2 us  [local(): lax.all_gather(proj, 'dp', axis=0, tiled=True)]
  transfers between devices with their start and end apart: 8 -> 8, of which waited for: 8 -> 8; matrix products, arithmetic and copies ran while one was open for 11% -> 8% of each run, Pallas kernels for 0% -> 0%
where the time goes in v1:
time: 1280 us
  waiting for transfers between devices  1090 us (85%)
  matrix products  72.8 us (6%)
  blocking collectives  49.5 us (4%)
  other arithmetic  28.3 us (2%)
  local copies, waits for them, and re-layouts  20.5 us (2%)
  between operations  14.3 us (1%)
    all_gather x1, waiting for transfers between devices, plan_field(): return jnp.sum(all_gather(sample, axis_name='tensor'), 0)  546 us
    reduce_scatter x1, waiting for transfers between devices, local(): lax.psum_scatter(jnp.dot(portion, w_out, preferred_element_type=jnp.float...  119 us
    all_gather x1, waiting for transfers between devices, local(): up_acts = add_rows(lax.all_gather(w_up, 'dp', axis=0, tiled=True))  95.4 us
    all_gather x1, waiting for transfers between devices, local(): gate_acts = add_rows(lax.all_gather(w_gate, 'dp', axis=0, tiled=True))  90.7 us
    all_gather x1, waiting for transfers between devices, local(): lax.all_gather(w_down, 'dp', axis=1, tiled=True)  81 us
    all_to_all x1, waiting for transfers between devices, local(): lax.all_to_all(lax.all_to_all(send_blocks, 'dp', split_axis=0, concat_axi...  60.9 us
    all_gather x1, waiting for transfers between devices, local(): gathered = lax.all_gather(student_in, 'tensor', axis=1, tiled=True)  59.9 us
    all_gather x1, waiting for transfers between devices, local(): lax.all_gather(proj, 'dp', axis=0, tiled=True)  36.2 us
  transfers between devices with their start and end apart: 8, of which 8 were waited for; matrix products, arithmetic and copies ran while one was open for 8% of the time, Pallas kernels for 0%

profile of v1, /device:TPU:0, one launch (start us, length us, event | category | flops | bytes accessed | tf_op | source)
XLA Modules:
  0.0 1283.0 jit_solution(9101830089235616560)
XLA Ops:
  10.0 16.8 %convolution_convert_fusion = bf16[512,8192]{1,0:T(8,128)(2,1)} fusion(bf16[512,1024]{1,0:T(8,128)(2,1)S(1)} %copy-done, bf16[1024,8192]{1,0:T(8,128)(2,1)} %param.12), kind=kOutput, calls=%fused_computation.5 | convolution fusion | flops 8594128896 | bytes 26214400 | tf_op jit(solution)/shard_map/dot_general | solution.py:33
  27.5 59.9 %all-gather.8.cloned.1.call-done = bf16[512,4096]{1,0:T(8,128)(2,1)} async-done(((bf16[512,512]{1,0:T(8,128)(2,1)}), bf16[512,4096]{1,0:T(8,128)(2,1)}) %all-gather.8.cloned.1.call-update) | async-done | bytes 4194320 | tf_op jit(solution)/shard_map/all_gather | solution.py:74
  87.4 3.1 fusion
  90.5 90.7 %all-gather.10.cloned.1.call-done = bf16[4096,1792]{1,0:T(8,128)(2,1)} async-done(((bf16[1024,1792]{1,0:T(8,128)(2,1)}), bf16[4096,1792]{1,0:T(8,128)(2,1)}) %all-gather.10.cloned.1.call-update) | async-done | bytes 14680080 | tf_op jit(solution)/shard_map/all_gather | solution.py:84
  181.2 14.6 %fusion.11 = f32[512,1792]{1,0:T(8,128)} fusion(bf16[4096,1792]{1,0:T(8,128)(2,1)} %all-gather.10.cloned.1.call-done, bf16[512,4096]{1,0:T(8,128)(2,1)} %all-gather.8.cloned.1.call-done, f32[4096]{0:T(1024)S(1)} %convert_element_type.49, f32[512]{0:T(512)S(1)} %add_rsqrt_fusion), kind=kOutput, calls=%fused_computation.23 | convolution fusion | flops 7524581376 | bytes 22562816 | tf_op jit(solution)/shard_map/dot_general | solution.py:82
  195.8 81.0 %all-gather.14.cloned.1.call-done = bf16[1792,4096]{1,0:T(8,128)(2,1)} async-done(((bf16[1792,1024]{1,0:T(8,128)(2,1)}), bf16[1792,4096]{1,0:T(8,128)(2,1)}) %all-gather.14.cloned.1.call-update) | async-done | bytes 14680080 | tf_op jit(solution)/shard_map/all_gather | solution.py:88
  276.8 95.4 %all-gather.12.cloned.1.call-done = bf16[4096,1792]{1,0:T(8,128)(2,1)} async-done(((bf16[1024,1792]{1,0:T(8,128)(2,1)}), bf16[4096,1792]{1,0:T(8,128)(2,1)}) %all-gather.12.cloned.1.call-update) | async-done | bytes 14680080 | tf_op jit(solution)/shard_map/all_gather | solution.py:85
  372.2 28.8 %convolution_convert_fusion.2 = bf16[512,4096]{1,0:T(8,128)(2,1)} fusion(bf16[1792,4096]{1,0:T(8,128)(2,1)} %all-gather.14.cloned.1.call-done, f32[512,1792]{1,0:T(8,128)} %fusion.11, bf16[4096,1792]{1,0:T(8,128)(2,1)} %all-gather.12.cloned.1.call-done, bf16[512,4096]{1,0:T(8,128)(2,1)} %all-gather.8.cloned.1.call-done, f32[4096]{0:T(1024)S(1)} %convert_element_type.49, ...), kind=kOutput, calls=%fused_computation.11 | convolution fusion | flops 15048376320 | bytes 41437184 | tf_op jit(solution)/shard_map/dot_general | solution.py:87
  402.0 1.7 select_reduce_fusion
  403.9 119.3 %reduce-scatter.2.cloned.1.call-done = bf16[64,8192]{1,0:T(8,128)(2,1)} async-done(((bf16[512,8192]{1,0:T(8,128)(2,1)}), bf16[64,8192]{1,0:T(8,128)(2,1)}) %reduce-scatter.2.cloned.1.call-update) | async-done | bytes 1048592 | tf_op jit(solution)/shard_map/reduce_scatter | solution.py:32
  524.9 2.0 convolution_convert_fusion.1
  529.5 28.2 %all_to_all.10 = bf16[4,8,32,1024]{3,2,1,0:T(8,128)(2,1)S(1)} all-to-all(bf16[4,8,32,1024]{3,2,1,0:T(8,128)(2,1)S(1)} %bitcast.19), channel_id=1, replica_groups=mesh['dp'=4,'tensor'=8] {'dp'}, dimensions={0} | all-to-all | bytes 4194304 | tf_op jit(solution)/shard_map/all_to_all | solution.py:63
  559.1 4.4 all-to-all-start.1
  563.7 8.3 scatter_custom_fusion
  572.2 60.9 %all-to-all-done.1 = bf16[4,8,32,1024]{3,2,0,1:T(8,128)(2,1)} async-done(((bf16[4,8,32,1024]{3,2,0,1:T(8,128)(2,1)}), bf16[4,8,32,1024]{3,2,0,1:T(8,128)(2,1)}, u32[]{:S(2)}, u32[]{:S(2)}) %all-to-all-start.1) | async-done | bytes 2097184 | tf_op jit(solution)/shard_map/all_to_all | solution.py:62
  633.0 1.8 copy.34
  634.9 2.8 gather_fusion
  637.6 546.2 %all-gather.18.cloned.1.call-done = bf16[4096,4096]{1,0:T(8,128)(2,1)} async-done(((bf16[512,4096]{1,0:T(8,128)(2,1)}), bf16[4096,4096]{1,0:T(8,128)(2,1)}) %all-gather.18.cloned.1.call-update) | async-done | bytes 33554448 | tf_op jit(solution)/shard_map/all_gather | solution.py:11
  1183.8 15.8 %reduce_sum.49 = bf16[512,4096]{1,0:T(8,128)(2,1)} reduce(bf16[8,512,4096]{2,1,0:T(8,128)(2,1)} %bitcast.16, bf16[]{:T(256)} %constant.63.clone.1), dimensions={0}, to_apply=%region_1.0 | reduce | flops 14680064 | bytes 37748736 | tf_op jit(solution)/shard_map/reduce_sum | solution.py:11
  1199.6 5.1 fusion.3
  1204.7 1.9 copy-done.2
  1207.5 36.2 %all-gather.16.cloned.1.call-done = bf16[4096,1024]{1,0:T(8,128)(2,1)} async-done(((bf16[1024,1024]{1,0:T(8,128)(2,1)}), bf16[4096,1024]{1,0:T(8,128)(2,1)}) %all-gather.16.cloned.1.call-update) | async-done | bytes 8388624 | tf_op jit(solution)/shard_map/all_gather | solution.py:97
  1243.7 10.6 multiply_reduce_fusion
  1254.3 21.3 %psum.7 = f32[512]{0:T(512)S(1)} all-reduce(f32[512]{0:T(512)S(1)} %get-tuple-element.7), channel_id=1, replica_groups=mesh['dp'=4,'tensor'=8] {'tensor'}, use_global_device_ids=true, to_apply=%region_8.9 | all-reduce | flops 512 | bytes 4096 | tf_op jit(solution)/shard_map/psum | solution.py:101
  (49 shorter events, 12.0 us)
Async XLA Ops:
  7.2 2.9 copy-start
  7.2 80.2 %all-gather.8.cloned.1.call-start = ((), (), s32[]{:S(2)}) async-start(), calls=%async_computation.3 | async-start | bytes 4718592 | tf_op jit(solution)/shard_map/all_gather | solution.py:74
  7.9 173.3 %all-gather.10.cloned.1.call-start = ((), (), s32[]{:S(2)}) async-start(), calls=%async_computation.4 | async-start | bytes 18350080 | tf_op jit(solution)/shard_map/all_gather | solution.py:84
  8.7 268.1 %all-gather.14.cloned.1.call-start = ((), (), s32[]{:S(2)}) async-start(), calls=%async_computation.6 | async-start | bytes 18350080 | tf_op jit(solution)/shard_map/all_gather | solution.py:88
  9.4 362.8 %all-gather.12.cloned.1.call-start = ((), (), s32[]{:S(2)}) async-start(), calls=%async_computation.5 | async-start | bytes 18350080 | tf_op jit(solution)/shard_map/all_gather | solution.py:85
  10.0 513.2 %reduce-scatter.2.cloned.1.call-start = ((), (), s32[]{:S(2)}) async-start(), calls=%async_computation.8 | async-start | bytes 9437184 | tf_op jit(solution)/shard_map/reduce_scatter | solution.py:32
  26.8 0.7 copy-start.6
  26.8 1157.0 %all-gather.18.cloned.1.call-start = ((), (), s32[]{:S(2)}) async-start(), calls=%async_computation.9 | async-start | bytes 37748736 | tf_op jit(solution)/shard_map/all_gather | solution.py:11
  401.0 0.8 copy-start.5
  401.0 0.8 copy-start.7
  401.0 122.2 %copy-start.3 = (bf16[64,8192]{1,0:T(8,128)(2,1)S(1)}, bf16[64,8192]{1,0:T(8,128)(2,1)}, u32[]{:S(2)}) copy-start(bf16[64,8192]{1,0:T(8,128)(2,1)} %param.13) | copy-start | bytes 3145732
  401.1 842.6 %all-gather.16.cloned.1.call-start = ((), (), s32[]{:S(2)}) async-start(), calls=%async_computation.7 | async-start | bytes 10485760 | tf_op jit(solution)/shard_map/all_gather | solution.py:97
  559.1 73.9 %all-to-all-start.1 = ((bf16[4,8,32,1024]{3,2,0,1:T(8,128)(2,1)}), bf16[4,8,32,1024]{3,2,0,1:T(8,128)(2,1)}, u32[]{:S(2)}, u32[]{:S(2)}) async-start(bf16[4,8,32,1024]{3,2,0,1:T(8,128)(2,1)} %copy.33), calls=%async_computation.2 | async-start | bytes 4194304 | tf_op jit(solution)/shard_map/all_to_all | solution.py:62
  1199.6 44.0 %copy-start.4 = (bf16[512,1024]{1,0:T(8,128)(2,1)S(1)}, bf16[512,1024]{1,0:T(8,128)(2,1)}, u32[]{:S(2)}) copy-start(bf16[512,1024]{1,0:T(8,128)(2,1)} %gather_fusion) | copy-start | bytes 3145732
  1204.7 1.9 copy-start.2
  1243.7 32.5 %copy-start.1 = (bf16[512,1024]{1,0:T(8,128)(2,1)S(1)}, bf16[512,1024]{1,0:T(8,128)(2,1)}, u32[]{:S(2)}) copy-start(bf16[512,1024]{1,0:T(8,128)(2,1)} %param.11) | copy-start | bytes 3145732
Sparse Core Ops, SparseCore 0:
  10.0 77.3 all-gather.7
  89.0 92.1 all-gather.9
  182.8 93.9 all-gather.13
  278.2 93.9 all-gather.11
  375.7 147.4 reduce-scatter.1
  524.6 659.2 all-gather.17
  1185.4 58.2 all-gather.15
